TPU v7x, 32 devices: a whole 2x2x4 slice. The times are simulated.
32 devices in a mesh: data: 2 (over x), hid: 4 (over z), vocab: 4 (over y, core).
Axes of the slice: x: 2, y: 2, z: 4, core: 2. Of those that a mesh axis runs over, the one named last changes fastest.
Arguments:
- h_states: bfloat16 [2048, 2048], P('data', 'hid'), parts along dimension 0
- w_head: bfloat16 [2048, 100352], P('hid', 'vocab')
- inv_temp: float32 [2048], P('data'), parts along dimension 0
- tgt_ids: int32 [2048], P('data'), parts along dimension 0
Outputs:
- output 1: float32 [2048, 100352], P('data', ('vocab', 'hid')), parts along dimension 0
- output 2: float32 [2048], P('data'), parts along dimension 0
There are 2 independent parts. A program takes and returns all parts, laid end to end along the dimension named above; an argument that names none is the same for every part.
All inputs are finite; a program needn't handle non-finite values.
Results may differ from a plain program's by a relative error of at most 0.001.
Values are sent between devices in bfloat16 or wider.
A program may use at most 1 GiB of HBM per device.

v0:
```python
import functools

import jax
import jax.numpy as jnp
from jax import lax
from jax.experimental import pallas as pl
from jax.experimental.pallas import tpu as pltpu
from jax.sharding import PartitionSpec as P

MESH = pl.DeviceIdType.MESH
F32 = jnp.float32
BF16 = jnp.bfloat16
TILE = 256
LANES = 128
SLOTS = 32
LOWEST = float(jnp.finfo(jnp.float32).min)


def tiles_of(blocks):
    whole = (blocks - 3) // 2
    tiles = [(t * TILE, TILE) for t in range(whole)]
    return tiles + [(b * LANES, LANES) for b in range(2 * whole, blocks)]


def chunks_of(blocks):
    whole = (blocks - 3) // 2
    sizes, left = [], 2 * whole - 2
    for size in (2, 2, 2, 2, 4, 4):
        if left > size:
            sizes.append(size)
            left -= size
    while left > 0:
        sizes.append(min(6, left))
        left -= sizes[-1]
    plan, at = [], 0
    for size in reversed(sizes):
        plan.append((at, size, 0, 2))
        at += size
    plan += [(b, 1, 0, 2) for b in range(at, blocks - 2)]
    return plan + [(b, 1, r, 1) for b in (blocks - 2, blocks - 1) for r in (0, 1)]


def service_order(plan, blocks):
    events = [(0.15 * blocks, "h line", 0), (0.28 * blocks, "h chip", 0)]
    for j, (first, size, _, _) in enumerate(plan):
        end = first + size
        events.append((first + size / 3 + 2, 0, j))
        events.append((end + 2, 2, j))
        events.append((min(1.86 * end, 0.68 * blocks + 0.6 * end) + 2, 1, j))
    events.sort(key=lambda e: e[0])
    order = [e[1:] for e in events]
    for j in range(len(plan)):
        at = max(order.index((k, j)) for k in (0, 1, 2))
        order.remove((1, j))
        order.insert(at, (1, j))
    return order


def folds_of(plan, first_end):
    folds, at = [], 0
    for j in (first_end // 3, 3 * first_end // 5):
        stop = sum(plan[j][:2]) // 2 - 1
        if j < first_end and stop > at:
            folds.append((j, at, stop))
            at = stop
    return folds


def split3(e):
    hi = e.astype(BF16)
    rest = e - hi.astype(F32)
    mid = rest.astype(BF16)
    low = (rest - mid.astype(F32)).astype(BF16)
    return hi, mid, low


def prefix_kernel(
    n_cols, h_ref, w_ref, temp_hbm, tgt_hbm,
    c_ref, coef_ref, factor_ref, tgt_out_ref,
    wbuf, hbuf, zbuf, tri, tri_last, stats, t_all, temp_col, rel_col, temp_ref, tgt_ref, zmsg, vmsg, back,
    ws, wr, xs, xr, ts, tr, wl, hl, hs, hr, zs, zr, vs, vr, rl,
):
    x, z, v = lax.axis_index("data"), lax.axis_index("hid"), lax.axis_index("vocab")
    rows, depth = h_ref.shape
    half, quarter = depth // 2, rows // 4
    tiles = tiles_of(n_cols // LANES)
    n_tiles = len(tiles)
    n_whole = sum(width == TILE for _, width in tiles)
    plan = chunks_of(n_cols // LANES)
    n_chunks = len(plan)
    ends = [[j for j, (first, *_) in enumerate(plan) if first * LANES < sum(tiles[t])][-1] for t in range(n_whole - 1, n_tiles)]
    first_end = ends[0] - 1

    side = z // 2
    outer_far, inner_far, near = 3 - 3 * side, 2 - side, 1 - z + 4 * side
    is_outer = jnp.where(z == side * 3, 1, 0)
    z_two, z_one = lax.rem(z + 2, 4), near
    v_two, v_one = lax.rem(v + 2, 4), v + 1 - 2 * lax.rem(v, 2)
    sources = (near, inner_far, outer_far)

    def cols_of(j):
        first, size, _, _ = plan[j]
        return first * LANES, size * LANES

    def w_rows(source, part, j=None):
        at, n = (0, half) if j is None else (plan[j][2] * (half // 2), plan[j][3] * (half // 2))
        return pl.ds(pl.multiple_of(source * depth + part * half + at, half // 2), n)

    def w_place(j, source, part):
        start, n = cols_of(j)
        return wbuf.at[w_rows(source, part, j), pl.ds(start, n)]

    def h_place(q, block=None):
        at = pl.ds(pl.multiple_of(q * quarter, quarter), quarter)
        if block is None:
            return hbuf.at[at]
        return hbuf.at[at, pl.ds(pl.multiple_of(block * depth, depth), depth)]

    def remote(src, dst, send, recv, **to):
        return pltpu.make_async_remote_copy(
            src_ref=src, dst_ref=dst, send_sem=send, recv_sem=recv, device_id=to, device_id_type=MESH
        )

    def w_source(j, part, dest):
        start, n = cols_of(j)
        return w_ref.at[w_rows(0, part, j), pl.ds(pl.multiple_of(dest * n_cols + start, LANES), n)]

    def direct(j, k, dest, slot):
        return remote(w_source(j, x, dest), w_place(j, z, x), ws.at[k], wr.at[j, slot], hid=dest)

    def send_near(j):
        return direct(j, 0, near, 0)

    odd = lax.rem(v, 2)
    far_first = outer_far + odd * (inner_far - outer_far)
    far_second = inner_far + odd * (outer_far - inner_far)

    def send_far(j, i):
        return direct(j, 1 + i, (far_first, far_second)[i], 1 + is_outer)

    def send_twin(i):
        dest = (far_first, far_second)[i]
        return remote(w_source(n_chunks - 1, 1 - x, dest), w_place(n_chunks - 1, z, 1 - x), ts.at[i], tr, hid=dest)

    def twin_landed():
        place = w_place(n_chunks - 1, inner_far, 1 - x)
        remote(place, place, ts.at[0], tr, hid=inner_far).wait_recv()

    def landed(j, k):
        place = w_place(j, sources[k], x)
        remote(place, place, ws.at[k], wr.at[j, k], hid=sources[k]).wait_recv()

    def forward(j, k):
        place = w_place(j, sources[k], x)
        send = 3 if k == 1 and j == n_chunks - 2 else k
        return remote(place, place, xs.at[send], xr.at[cross(j, k)], data=1 - x)

    def cross(j, k):
        if j < first_end:
            return j
        return first_end if k != 1 else 1 + j

    def cross_wait(slot, count, start, stop):
        place = wbuf.at[pl.ds(0, count), pl.ds(start, stop - start)]
        remote(place, place, xs.at[0], xr.at[slot], data=1 - x).wait_recv()

    def forwarded(j):
        place = w_place(j, inner_far, 1 - x)
        remote(place, place, xs.at[1], xr.at[cross(j, 1)], data=1 - x).wait_recv()

    def own(j):
        start, n = cols_of(j)
        return pltpu.make_async_copy(
            w_ref.at[:, pl.ds(pl.multiple_of(z * n_cols + start, LANES), n)],
            wbuf.at[pl.ds(pl.multiple_of(z * depth, depth), depth), pl.ds(start, n)],
            wl,
        )

    h_mine = h_ref.at[pl.ds(pl.multiple_of(v * quarter, quarter), quarter)]
    h_own = pltpu.make_async_copy(h_mine, h_place(v, z), hl)
    h_two = remote(h_mine, h_place(v, z), hs, hr.at[0], hid=z_two)
    h_one = remote(h_mine, h_place(v, z), hs, hr.at[1], hid=z_one)
    h_relay = remote(h_place(v, z_two), h_place(v, z_two), hs, hr.at[2], hid=z_one)
    h_chip = remote(h_place(v), h_place(v), hs, hr.at[3], vocab=v_two)
    h_core = remote(h_place(v), h_place(v), hs, hr.at[4], vocab=v_one)
    h_both = remote(h_place(v_two), h_place(v_two), hs, hr.at[5], vocab=v_one)

    def arrived(place, i, **frm):
        remote(place, place, hs, hr.at[i], **frm).wait_recv()

    barrier = pltpu.get_barrier_semaphore()
    peers = [{"hid": outer_far}, {"hid": inner_far}, {"hid": near}, {"data": 1 - x}]
    peers += [{"vocab": lax.rem(v + d, 4)} for d in (2, 1, 3)]
    for peer in peers:
        pl.semaphore_signal(barrier, inc=1, device_id=peer, device_id_type=MESH)
    row_copies = [
        pltpu.make_async_copy(temp_hbm, temp_ref, rl.at[0]),
        pltpu.make_async_copy(tgt_hbm, tgt_ref, rl.at[1]),
    ]
    for copy in (h_own, *row_copies):
        copy.start()
    for j in range(n_chunks):
        if plan[j][2] == 0:
            own(j).start()
    with jax.named_scope("bar"):
        pl.semaphore_wait(barrier, len(peers))

    h_two.start()
    h_one.start()
    send_near(0).start()
    send_far(0, 0).start()

    def ones_below(ref, width):
        k = lax.broadcasted_iota(jnp.int32, (width, width), 0)
        c = lax.broadcasted_iota(jnp.int32, (width, width), 1)
        block = jnp.where(k <= c, 1.0, 0.0).astype(BF16)
        for i in range(3):
            ref[pl.ds(i * width, width), :] = block

    ones_below(tri, TILE)
    ones_below(tri_last, LANES)
    base = (v * 4 + z) * n_cols
    for copy in row_copies:
        copy.wait()
    back[0:1, :] = temp_ref[...]
    back[1:2, :] = (tgt_ref[...] - base).astype(F32)
    cols8 = back[...].T
    temp_col[...] = jnp.broadcast_to(cols8[:, 0:1], temp_col.shape)
    rel_col[...] = jnp.broadcast_to(cols8[:, 1:2], rel_col.shape).astype(jnp.int32)
    slot = lax.broadcasted_iota(jnp.int32, stats.shape, 1)
    stats[...] = jnp.where(slot < SLOTS, LOWEST, 0.0)
    t_all[...] = jnp.zeros(t_all.shape, F32)

    with jax.named_scope("h0"):
        arrived(h_place(v, z_two), 0, hid=z_two)
    h_relay.start()
    send_far(0, 1).start()
    for j in range(1, n_chunks):
        send_near(j).start()
        send_far(j, 0).start()
        send_far(j, 1).start()

    @pl.when(is_outer == 0)
    def _():
        send_twin(0).start()
        send_twin(1).start()


    part, few = min(rows, 512), min(rows, 128)

    def logits_and_sums(product, sums):
        some = part if product is not None or sums[2] == TILE else min(rows, 2 * part)

        @pl.loop(0, rows // some)
        def _(i):
            if product is not None:
                _, new_start, new_width = product
                at = pl.ds(pl.multiple_of(i * part, part), part)
                new = jnp.dot(
                    hbuf[at, :], wbuf[:, pl.ds(new_start, new_width)], preferred_element_type=F32
                )
            for k in range(0, some, few) if sums is not None else ():
                prefix(pl.ds(pl.multiple_of(i * some + k, few), few), *sums)
            if product is not None:
                zbuf[at, 0:new_width] = new

    def prefix(at, t, start, width, ending=False):
        pieces = width // LANES
        logits = zbuf[at, 0:width] * jnp.concatenate([temp_col[at, :]] * pieces, axis=1)
        lane = lax.broadcasted_iota(jnp.int32, (few, LANES), 1)
        top = jnp.max(logits, axis=1, keepdims=True)
        e = jnp.exp(logits - top)
        total = jnp.sum(e, axis=1, keepdims=True)
        old = stats[at, :]
        table = tri if width == TILE else tri_last
        run = jnp.dot(jnp.concatenate(split3(e), axis=1), table[...], preferred_element_type=F32)
        c_ref[at, pl.ds(start, width)] = run
        rel = rel_col[at, :] - start
        if ending:
            hit = jnp.where(lane == rel, run, 0.0)
            old = jnp.where(lane == 2 * SLOTS, old + jnp.sum(hit, axis=1, keepdims=True), old)
        else:
            hit = t_all[at, :]
            for p in range(pieces):
                hit += jnp.where(lane == rel - p * LANES, run[:, p * LANES : (p + 1) * LANES], 0.0)
            t_all[at, :] = hit
        stats[at, :] = jnp.where(lane == t, top, jnp.where(lane == SLOTS + t, total, old))

    def collect():
        lane = lax.broadcasted_iota(jnp.int32, stats.shape, 1)
        stats[...] = jnp.where(lane == 2 * SLOTS, jnp.sum(t_all[...], axis=1, keepdims=True), stats[...])

    def whole(t):
        return t, pl.multiple_of(t * TILE, TILE), TILE

    def compute(j):
        first, size = (n // 2 for n in plan[j][:2])
        stop = first + size
        if first == 0:
            logits_and_sums(whole(0), None)
            first = 1
        if first < stop:

            @pl.loop(first, stop)
            def _(t):
                logits_and_sums(whole(t), whole(t - 1))

        if j == first_end - 1:
            logits_and_sums(None, whole(stop - 1))

    def block_dot(at, block, start, width):
        lanes = pl.ds(pl.multiple_of(block * depth, depth), depth)
        return jnp.dot(hbuf[at, lanes], wbuf[lanes, start : start + width], preferred_element_type=F32)

    def begin_end(i):
        start, width = tiles[n_whole - 1 + i]

        @pl.loop(0, rows // part)
        def _(k):
            at = pl.ds(pl.multiple_of(k * part, part), part)
            c_ref[at, start : start + width] = (
                block_dot(at, z, start, width)
                + block_dot(at, near, start, width)
                + block_dot(at, outer_far, start, width)
            )

    def finish_end(i):
        t = n_whole - 1 + i
        start, width = tiles[t]
        every = slice(0, rows)
        zbuf[:, 0:width] = c_ref[:, start : start + width] + block_dot(every, inner_far, start, width)
        logits_and_sums(None, (t, start, width, t == n_tiles - 1))

    def fold(g0, g1):
        @pl.loop(0, rows // few)
        def _(i):
            at = pl.ds(pl.multiple_of(i * few, few), few)
            lane = lax.broadcasted_iota(jnp.int32, (few, LANES), 1)
            group = (lane >= g0) & (lane < g1)
            m = stats[at, :]
            s = pltpu.roll(m, LANES - SLOTS, 1)
            top = jnp.max(jnp.where(group, m, LOWEST), axis=1, keepdims=True)
            shrink = jnp.where(group, jnp.exp(m - top), 0.0)
            parts = jnp.where(group, s, 0.0) * shrink
            before = prefix_before(parts)
            for t in range(g0, g1):
                span = slice(t * TILE, (t + 1) * TILE)
                c_ref[at, span] = c_ref[at, span] * shrink[:, t : t + 1] + before[:, t : t + 1]
            rel = rel_col[at, :]
            holds = (rel >= lane * TILE) & (rel < (lane + 1) * TILE)
            old = t_all[at, :]
            moved = jnp.sum(old, axis=1, keepdims=True) * shrink + before
            inside = (rel >= g0 * TILE) & (rel < g1 * TILE)
            t_all[at, :] = jnp.where(inside, jnp.where(holds, moved, 0.0), old)
            total = jnp.sum(parts, axis=1, keepdims=True)
            sums = jnp.where(lane == SLOTS + g1 - 1, total, 0.0)
            of_sums = (lane >= SLOTS + g0) & (lane < SLOTS + g1)
            stats[at, :] = jnp.where(group, top, jnp.where(of_sums, sums, m))

    def close(i):
        first = ends[i - 1] + 1 if i else first_end
        with jax.named_scope(f"xe{i}"):
            for j in range(first, ends[i] + 1):
                if j < n_chunks - 1:
                    forwarded(j)
                else:
                    twin_landed()
        with jax.named_scope(f"ce{i}"):
            finish_end(i)

    def prefix_before(parts):
        k = lax.broadcasted_iota(jnp.int32, (LANES, LANES), 0)
        c = lax.broadcasted_iota(jnp.int32, (LANES, LANES), 1)
        strict = jnp.where(k < c, 1.0, 0.0).astype(BF16)
        return sum(jnp.dot(p, strict, preferred_element_type=F32) for p in split3(parts))

    def complete(j):
        start, n = cols_of(j)
        cross_wait(j, 3 * half, start, start + n)

    def own_complete():
        place = wbuf.at[pl.ds(pl.multiple_of(z * depth, depth), depth)]
        pltpu.make_async_copy(place, place, wl).wait()

    order = service_order(plan, n_cols // LANES)
    folds = {j: (g0, g1) for j, g0, g1 in folds_of(plan, first_end)}
    tail = range(first_end, n_chunks)
    known = max(order.index((k, j)) for k in (0, 2) for j in tail)
    early = min(j for j in range(max(0, first_end - 7), n_chunks - 1) if order.index((1, j + 1)) > known)
    assert early < first_end
    m = len(ends) - 1
    closes = {n_chunks - 3: range(m - 2), n_chunks - 2: [m - 2], n_chunks - 1: [m - 1]}

    for what, j in order:
        if what == "h line":
            with jax.named_scope("hline"):
                arrived(h_place(v, z_one), 1, hid=z_one)
                arrived(h_place(v, lax.rem(z_one + 2, 4)), 2, hid=z_one)
                h_own.wait()
            h_chip.start()
            h_core.start()
        elif what == "h chip":
            with jax.named_scope("hchip"):
                arrived(h_place(v_two), 3, vocab=v_two)
            h_both.start()
        else:
            with jax.named_scope(f"w{what}_{j}"):
                landed(j, what)
            if (what, j) != (1, n_chunks - 1):
                forward(j, what).start()
            if what != 1:
                continue
            if j == 1:
                with jax.named_scope("hcore"):
                    arrived(h_place(v_one), 4, vocab=v_one)
                    arrived(h_place(lax.rem(v_one + 2, 4)), 5, vocab=v_one)
                    own_complete()
            if 0 < j <= first_end:
                with jax.named_scope(f"x{j - 1}"):
                    complete(j - 1)
                with jax.named_scope(f"c{j - 1}"):
                    compute(j - 1)
                if j - 1 in folds:
                    with jax.named_scope(f"f{j - 1}"):
                        fold(*folds[j - 1])
            if j - 1 == early:
                with jax.named_scope("begin"):
                    cross_wait(first_end, 2 * half, cols_of(first_end)[0], n_cols)
                    for i in range(len(ends)):
                        begin_end(i)
            for i in closes.get(j, ()):
                close(i)
    collect()
    close(m)

    lane = lax.broadcasted_iota(jnp.int32, (rows, LANES), 1)
    turned = stats[...].T
    m, at_tgt = turned[0:SLOTS, :], turned[2 * SLOTS : 2 * SLOTS + 1, :]
    top = jnp.max(m, axis=0, keepdims=True)
    shrink = jnp.exp(m - top)
    parts = turned[SLOTS : 2 * SLOTS, :] * shrink
    t = lax.broadcasted_iota(jnp.int32, (SLOTS, rows), 0)
    start = jnp.where(t < n_whole, t * TILE, n_whole * (TILE - LANES) + t * LANES)
    stop = start + jnp.where(t < n_whole, TILE, LANES)
    rel = tgt_ref[...] - base
    known = rel < n_cols
    holds = (rel >= start) & (rel < stop) & known
    ahead = (stop <= rel) & known
    found = jnp.where(holds, at_tgt * shrink, jnp.where(ahead, parts, 0.0))
    zmsg[z, 0:1, :] = top
    zmsg[z, 1:2, :] = jnp.sum(parts, axis=0, keepdims=True)
    zmsg[z, 2:3, :] = jnp.sum(found, axis=0, keepdims=True)

    for k in range(3):
        mine = wbuf.at[w_rows(sources[k], x)]
        remote(mine, mine, ws.at[k], wr.at[0, k], hid=near).wait_send()
        if k == 1:
            mine = wbuf.at[w_rows(sources[k], x), pl.ds(0, n_cols - LANES)]
        remote(mine, mine, xs.at[k], xr.at[0], data=1 - x).wait_send()
    forward(n_chunks - 2, 1).wait_send()

    @pl.when(is_outer == 0)
    def _():
        send_twin(0).wait_send()
        send_twin(1).wait_send()

    mine = hbuf.at[pl.ds(0, quarter * 15 // 4)]
    remote(mine, mine, hs, hr.at[0], hid=near).wait_send()

    def z_send(i):
        return remote(zmsg.at[z], zmsg.at[z], zs, zr, hid=(near, inner_far, outer_far)[i])

    def v_send(d):
        to = lax.rem(v + d, 4)
        return remote(vmsg.at[v], vmsg.at[v], vs, vr, vocab=to)

    for i in (2, 1, 0):
        z_send(i).start()
    k = lax.broadcasted_iota(jnp.int32, (SLOTS, SLOTS), 0)
    c = lax.broadcasted_iota(jnp.int32, (SLOTS, SLOTS), 1)
    strict = jnp.where(c < k, 1.0, 0.0).astype(BF16)
    before = sum(jnp.dot(strict, p, preferred_element_type=F32) for p in split3(parts))
    rest = jnp.zeros((LANES - 2 * SLOTS, rows), F32)
    coef_ref[...] = jnp.concatenate([shrink, before, rest], axis=0).T
    z_all = remote(zmsg.at[pl.ds(0, 3)], zmsg.at[pl.ds(0, 3)], zs, zr, hid=near)
    with jax.named_scope("z"):
        z_all.wait_recv()

    ids = tgt_ref[...]
    maxes = [zmsg[h, 0:1, :] for h in range(4)]
    v_max = functools.reduce(jnp.maximum, maxes)
    v_sum = jnp.zeros((1, rows), F32)
    v_tgt = jnp.zeros((1, rows), F32)
    mine_before = jnp.zeros((1, rows), F32)
    for h in range(4):
        mine_before = jnp.where(h == z, v_sum, mine_before)
        f = jnp.exp(maxes[h] - v_max)
        low = (v * 4 + h) * n_cols
        inside = (ids >= low) & (ids < low + n_cols)
        v_tgt += jnp.where(inside, zmsg[h, 2:3, :] * f + v_sum, 0.0)
        v_sum += zmsg[h, 1:2, :] * f
    vmsg[v, 0:1, :] = v_max
    vmsg[v, 1:2, :] = v_sum
    vmsg[v, 2:3, :] = v_tgt

    z_all.wait_send()
    for d in (2, 1, 3):
        v_send(d).start()
    v_all = remote(vmsg.at[pl.ds(0, 3)], vmsg.at[pl.ds(0, 3)], vs, vr, vocab=v_one)
    with jax.named_scope("v"):
        v_all.wait_recv()

    maxes = [vmsg[u, 0:1, :] for u in range(4)]
    g_max = functools.reduce(jnp.maximum, maxes)
    g_sum = jnp.zeros((1, rows), F32)
    g_tgt = jnp.zeros((1, rows), F32)
    g_before = jnp.zeros((1, rows), F32)
    for u in range(4):
        f = jnp.exp(maxes[u] - g_max)
        g_before = jnp.where(u == v, g_sum + mine_before * f, g_before)
        low = u * 4 * n_cols
        inside = (ids >= low) & (ids < low + 4 * n_cols)
        g_tgt += jnp.where(inside, vmsg[u, 2:3, :] * f + g_sum, 0.0)
        g_sum += vmsg[u, 1:2, :] * f
    tgt_out_ref[...] = g_tgt / g_sum
    factor_ref[0:1, :] = jnp.exp(zmsg[z, 0:1, :] - g_max) / g_sum
    factor_ref[1:2, :] = g_before / g_sum
    v_all.wait_send()


def finish_kernel(tiles, lanes, c_ref, coef_ref, factor_ref, tgt_ref, out_ref, tgt_out_ref, buf, factor_col, sems, tgt_sem):
    slots, n, n_cols = buf.shape
    steps = c_ref.shape[0] // n
    tgt_copy = pltpu.make_async_copy(tgt_ref, tgt_out_ref, tgt_sem)
    tgt_copy.start()

    def put(i):
        slot = lax.rem(i, slots)
        at = pl.ds(pl.multiple_of(i * n, n), n)
        return pltpu.make_async_copy(buf.at[slot], out_ref.at[at], sems.at[slot])

    @pl.loop(0, steps)
    def _(i):
        slot = lax.rem(i, slots)

        @pl.when(i >= slots)
        def _():
            put(i - slots).wait()

        at = pl.ds(pl.multiple_of(i * n, n), n)
        turn = max(n, LANES)

        @pl.when(lax.rem(i, turn // n) == 0)
        def _():
            some = pl.ds(pl.multiple_of(i // (turn // n) * turn, turn), turn)
            factor_col[some, :] = factor_ref[:, some].T

        lane = lax.broadcasted_iota(jnp.int32, (n, LANES), 1)
        coef = coef_ref[at, :] * factor_col[at, 0:1] + jnp.where(lane < SLOTS, 0.0, factor_col[at, 1:2])
        for (start, width), k in zip(tiles, lanes):
            span = slice(start, start + width)
            buf[slot, :, span] = c_ref[at, span] * coef[:, k : k + 1] + coef[:, SLOTS + k : SLOTS + k + 1]
        put(i).start()

    tgt_copy.wait()
    for i in range(max(0, steps - slots), steps):
        with jax.named_scope(f"fe{i}"):
            put(i).wait()


def solution(mesh):
    n_hid, n_voc = mesh.shape["hid"], mesh.shape["vocab"]
    assert n_hid == 4 and n_voc == 4 and mesh.shape["data"] == 2

    def local_step(h_blk, w_blk, temp_blk, tgt_blk):
        rows, depth = h_blk.shape
        n_cols = w_blk.shape[1] // n_hid
        assert n_cols % LANES == 0
        tiles = tiles_of(n_cols // LANES)
        n_tiles = len(tiles)
        assert n_tiles <= SLOTS
        plan = chunks_of(n_cols // LANES)
        n_chunks = len(plan)
        last_whole = sum(width == TILE for _, width in tiles) - 1
        first_end = [first for first, *_ in plan].index(2 * last_whole)
        vmem = pl.BlockSpec(memory_space=pltpu.VMEM)
        hbm = pl.BlockSpec(memory_space=pltpu.HBM)
        dma = pltpu.SemaphoreType.DMA
        table = pltpu.VMEM((rows, LANES), F32)
        c, coef, factor, tgt = pl.pallas_call(
            functools.partial(prefix_kernel, n_cols),
            out_shape=(
                pltpu.VMEM((rows, n_cols), F32),
                pltpu.VMEM((rows, LANES), F32),
                pltpu.VMEM((8, rows), F32),
                pltpu.VMEM((1, rows), F32),
            ),
            in_specs=[hbm] * 4,
            out_specs=[vmem] * 4,
            scratch_shapes=[
                pltpu.VMEM((4 * depth, n_cols), BF16),
                pltpu.VMEM((rows, 4 * depth), BF16),
                pltpu.VMEM((rows, TILE), F32),
                pltpu.VMEM((3 * TILE, TILE), BF16),
                pltpu.VMEM((3 * LANES, LANES), BF16),
                table,
                table,
                table,
                pltpu.VMEM((rows, LANES), jnp.int32),
                pltpu.VMEM((1, rows), F32),
                pltpu.VMEM((1, rows), jnp.int32),
                pltpu.VMEM((4, 3, rows), F32),
                pltpu.VMEM((4, 3, rows), F32),
                pltpu.VMEM((8, rows), F32),
                dma((3,)),
                dma((n_chunks, 3)),
                dma((4,)),
                dma((n_chunks,)),
                dma((2,)),
                dma,
                dma,
                dma,
                dma,
                dma((6,)),
                dma,
                dma,
                dma,
                dma,
                dma((2,)),
            ],
            compiler_params=pltpu.CompilerParams(
                collective_id=0, has_side_effects=True, vmem_limit_bytes=37 << 20
            ),
            name="prefix",
        )(h_blk, w_blk, temp_blk.reshape(1, rows), tgt_blk.reshape(1, rows))
        n = min(rows, 64)
        lanes = list(range(n_tiles))
        for _, g0, g1 in folds_of(plan, first_end):
            lanes[g0:g1] = [g0] * (g1 - g0)
        cdf, cdf_tgt = pl.pallas_call(
            functools.partial(finish_kernel, tiles, lanes),
            out_shape=(
                jax.ShapeDtypeStruct((rows, n_cols), F32),
                jax.ShapeDtypeStruct((1, rows), F32),
            ),
            in_specs=[vmem] * 4,
            out_specs=[hbm, hbm],
            scratch_shapes=[
                pltpu.VMEM((4, n, n_cols), F32),
                pltpu.VMEM((rows, 8), F32),
                dma((4,)),
                dma,
            ],
            compiler_params=pltpu.CompilerParams(vmem_limit_bytes=9 << 20),
            name="finish",
        )(c, coef, factor, tgt)
        return cdf, cdf_tgt.reshape(rows)

    return jax.shard_map(
        local_step,
        mesh=mesh,
        in_specs=(P("data", "hid"), P("hid", "vocab"), P("data"), P("data")),
        out_specs=(P("data", ("vocab", "hid")), P("data")),
        check_vma=False,
    )
```

profile of v0, /device:TPU:0, one launch (start us, length us, event | category | flops | bytes accessed | tf_op | source)
XLA Modules:
  0.0 313.5 jit_solution(3456908301252042239)
XLA Ops:
  0.6 303.5 %prefix.1 = (f32[1024,6272]{1,0:T(8,128)S(1)}, f32[1024,128]{1,0:T(8,128)S(1)}, f32[8,1024]{1,0:T(8,128)S(1)}, f32[1,1024]{1,0:T(1,128)S(1)}) custom-call(bf16[1024,512]{1,0:T(8,128)(2,1)} %h_ref.1, bf16[512,25088]{1,0:T(8,128)(2,1)} %w_ref.1, f32[1,1024]{1,0:T(1,128)} %bitcast.3, s32[1,1024]{1,0:T(1,128)} %bitcast.4), custom_call_target="tpu_custom_call" | custom-call | tf_op jit(solution)/shard_map/prefix/pallas_call | solution.py:590
  304.2 9.1 %finish.1 = (f32[1024,6272]{1,0:T(8,128)}, f32[1,1024]{1,0:T(1,128)}) custom-call(f32[1024,6272]{1,0:T(8,128)S(1)} %get-tuple-element.8.c_ref, f32[1024,128]{1,0:T(8,128)S(1)} %get-tuple-element.9.coef_ref, f32[8,1024]{1,0:T(8,128)S(1)} %get-tuple-element.10.factor_ref, f32[1,1024]{1,0:T(1,128)S(1)} %get-tuple-element.11.tgt_ref), custom_call_target="tpu_custom_call" | custom-call | tf_op jit(solution)/shard_map/finish/pallas_call | solution.py:640
where the time goes:
time: 314 us; the launch traced here: 313 us
  Pallas kernels  313 us (100%)
    pallas_call x1, Pallas kernels, local_step(): pl.pallas_call(functools.partial(prefix_kernel, n_cols), out_shape=(pltpu...  304 us
    pallas_call x1, Pallas kernels, local_step(): pl.pallas_call(functools.partial(finish_kernel, tiles, lanes), out_shape=...  9.12 us

commit v1 on v0

--- a/solution.py
+++ b/solution.py
@@ -199,9 +199,6 @@
     ]
     for copy in (h_own, *row_copies):
         copy.start()
-    for j in range(n_chunks):
-        if plan[j][2] == 0:
-            own(j).start()
     with jax.named_scope("bar"):
         pl.semaphore_wait(barrier, len(peers))
 
@@ -209,6 +206,9 @@
     h_one.start()
     send_near(0).start()
     send_far(0, 0).start()
+    for j in range(n_chunks):
+        if plan[j][2] == 0:
+            own(j).start()
 
     def ones_below(ref, width):
         k = lax.broadcasted_iota(jnp.int32, (width, width), 0)

time: 314 us -> 314 us (level)
  no operation moved by 1% of the time
where the time goes in v1:
time: 314 us; the launch traced here: 313 us
  Pallas kernels  313 us (100%)
    pallas_call x1, Pallas kernels, local_step(): pl.pallas_call(functools.partial(prefix_kernel, n_cols), out_shape=(pltpu...  304 us
    pallas_call x1, Pallas kernels, local_step(): pl.pallas_call(functools.partial(finish_kernel, tiles, lanes), out_shape=...  9.12 us

profile of v1, /device:TPU:0, one launch (start us, length us, event | category | flops | bytes accessed | tf_op | source)
XLA Modules:
  0.0 313.5 jit_solution(1620200758898956046)
XLA Ops:
  0.6 303.5 %prefix.1 = (f32[1024,6272]{1,0:T(8,128)S(1)}, f32[1024,128]{1,0:T(8,128)S(1)}, f32[8,1024]{1,0:T(8,128)S(1)}, f32[1,1024]{1,0:T(1,128)S(1)}) custom-call(bf16[1024,512]{1,0:T(8,128)(2,1)} %h_ref.1, bf16[512,25088]{1,0:T(8,128)(2,1)} %w_ref.1, f32[1,1024]{1,0:T(1,128)} %bitcast.3, s32[1,1024]{1,0:T(1,128)} %bitcast.4), custom_call_target="tpu_custom_call" | custom-call | tf_op jit(solution)/shard_map/prefix/pallas_call | solution.py:590
  304.2 9.1 %finish.1 = (f32[1024,6272]{1,0:T(8,128)}, f32[1,1024]{1,0:T(1,128)}) custom-call(f32[1024,6272]{1,0:T(8,128)S(1)} %get-tuple-element.8.c_ref, f32[1024,128]{1,0:T(8,128)S(1)} %get-tuple-element.9.coef_ref, f32[8,1024]{1,0:T(8,128)S(1)} %get-tuple-element.10.factor_ref, f32[1,1024]{1,0:T(1,128)S(1)} %get-tuple-element.11.tgt_ref), custom_call_target="tpu_custom_call" | custom-call | tf_op jit(solution)/shard_map/finish/pallas_call | solution.py:640

commit v2 on v0

--- a/solution.py
+++ b/solution.py
@@ -481,7 +481,17 @@
     strict = jnp.where(c < k, 1.0, 0.0).astype(BF16)
     before = sum(jnp.dot(strict, p, preferred_element_type=F32) for p in split3(parts))
     rest = jnp.zeros((LANES - 2 * SLOTS, rows), F32)
-    coef_ref[...] = jnp.concatenate([shrink, before, rest], axis=0).T
+    spare = t == SLOTS - 1
+    coef_ref[...] = jnp.concatenate([jnp.where(spare, 1.0, shrink), jnp.where(spare, 0.0, before), rest], axis=0).T
+
+    @pl.loop(0, rows // few)
+    def _(i):
+        at = pl.ds(pl.multiple_of(i * few, few), few)
+        coef = coef_ref[at, :]
+        for q in range(folds_of(plan, first_end)[-1][2], n_whole):
+            span = slice(tiles[q][0], sum(tiles[q]))
+            c_ref[at, span] = c_ref[at, span] * coef[:, q : q + 1] + coef[:, SLOTS + q : SLOTS + q + 1]
+
     z_all = remote(zmsg.at[pl.ds(0, 3)], zmsg.at[pl.ds(0, 3)], zs, zr, hid=near)
     with jax.named_scope("z"):
         z_all.wait_recv()
@@ -528,38 +538,58 @@
     v_all.wait_send()
 
 
-def finish_kernel(tiles, lanes, c_ref, coef_ref, factor_ref, tgt_ref, out_ref, tgt_out_ref, buf, factor_col, sems, tgt_sem):
+def finish_kernel(tiles, lanes, c_ref, coef_ref, factor_ref, tgt_ref, out_ref, tgt_out_ref, buf, factor_col, sems, ends):
     slots, n, n_cols = buf.shape
     steps = c_ref.shape[0] // n
-    tgt_copy = pltpu.make_async_copy(tgt_ref, tgt_out_ref, tgt_sem)
+    turn = max(n, LANES)
+    tgt_copy = pltpu.make_async_copy(tgt_ref, tgt_out_ref, ends.at[2])
     tgt_copy.start()
 
     def put(i):
-        slot = lax.rem(i, slots)
         at = pl.ds(pl.multiple_of(i * n, n), n)
+        slot = lax.rem(i - 1, slots)
         return pltpu.make_async_copy(buf.at[slot], out_ref.at[at], sems.at[slot])
 
-    @pl.loop(0, steps)
-    def _(i):
-        slot = lax.rem(i, slots)
-
-        @pl.when(i >= slots)
-        def _():
-            put(i - slots).wait()
-
-        at = pl.ds(pl.multiple_of(i * n, n), n)
-        turn = max(n, LANES)
-
-        @pl.when(lax.rem(i, turn // n) == 0)
-        def _():
-            some = pl.ds(pl.multiple_of(i // (turn // n) * turn, turn), turn)
-            factor_col[some, :] = factor_ref[:, some].T
-
-        lane = lax.broadcasted_iota(jnp.int32, (n, LANES), 1)
+    def turn_factors(i):
+        some = pl.ds(pl.multiple_of(i // (turn // n) * turn, turn), turn)
+        factor_col[some, :] = factor_ref[:, some].T
+
+    def table(at, count, to):
+        lane = lax.broadcasted_iota(jnp.int32, (count, LANES), 1)
         coef = coef_ref[at, :] * factor_col[at, 0:1] + jnp.where(lane < SLOTS, 0.0, factor_col[at, 1:2])
         for (start, width), k in zip(tiles, lanes):
             span = slice(start, start + width)
-            buf[slot, :, span] = c_ref[at, span] * coef[:, k : k + 1] + coef[:, SLOTS + k : SLOTS + k + 1]
+            buf[(*to, span)] = c_ref[at, span] * coef[:, k : k + 1] + coef[:, SLOTS + k : SLOTS + k + 1]
+
+    turn_factors(0)
+    half = n // 2
+
+    def put_half(h):
+        at = pl.ds(pl.multiple_of(h * half, half), half)
+        return pltpu.make_async_copy(buf.at[slots - 1, at], out_ref.at[at], ends.at[h])
+
+    @pl.loop(0, 2)
+    def _(h):
+        at = pl.ds(pl.multiple_of(h * half, half), half)
+        table(at, half, (slots - 1, at))
+        put_half(h).start()
+
+    @pl.loop(1, steps)
+    def _(i):
+        @pl.when(i == slots)
+        def _():
+            put_half(0).wait()
+            put_half(1).wait()
+
+        @pl.when(i > slots)
+        def _():
+            put(i - slots).wait()
+
+        @pl.when(lax.rem(i, turn // n) == 0)
+        def _():
+            turn_factors(i)
+
+        table(pl.ds(pl.multiple_of(i * n, n), n), n, (lax.rem(i - 1, slots), slice(None)))
         put(i).start()
 
     tgt_copy.wait()
@@ -578,7 +608,7 @@
         assert n_cols % LANES == 0
         tiles = tiles_of(n_cols // LANES)
         n_tiles = len(tiles)
-        assert n_tiles <= SLOTS
+        assert n_tiles < SLOTS
         plan = chunks_of(n_cols // LANES)
         n_chunks = len(plan)
         last_whole = sum(width == TILE for _, width in tiles) - 1
@@ -633,10 +663,12 @@
             ),
             name="prefix",
         )(h_blk, w_blk, temp_blk.reshape(1, rows), tgt_blk.reshape(1, rows))
-        n = min(rows, 64)
+        n = min(rows // 8, 64)
+        assert rows // n > 4
         lanes = list(range(n_tiles))
         for _, g0, g1 in folds_of(plan, first_end):
             lanes[g0:g1] = [g0] * (g1 - g0)
+        lanes[g1 : last_whole + 1] = [SLOTS - 1] * (last_whole + 1 - g1)
         cdf, cdf_tgt = pl.pallas_call(
             functools.partial(finish_kernel, tiles, lanes),
             out_shape=(
@@ -649,7 +681,7 @@
                 pltpu.VMEM((4, n, n_cols), F32),
                 pltpu.VMEM((rows, 8), F32),
                 dma((4,)),
-                dma,
+                dma((3,)),
             ],
             compiler_params=pltpu.CompilerParams(vmem_limit_bytes=9 << 20),
             name="finish",

time: 314 us -> 313 us (level)
  no operation moved by 1% of the time
where the time goes in v2:
time: 313 us
  Pallas kernels  312 us (100%)
    pallas_call x1, Pallas kernels, local_step(): pl.pallas_call(functools.partial(prefix_kernel, n_cols), out_shape=(pltpu...  304 us
    pallas_call x1, Pallas kernels, local_step(): pl.pallas_call(functools.partial(finish_kernel, tiles, lanes), out_shape=...  8.94 us

profile of v2, /device:TPU:0, one launch (start us, length us, event | category | flops | bytes accessed | tf_op | source)
XLA Modules:
  0.0 313.3 jit_solution(822684977504753690)
XLA Ops:
  0.6 303.6 %prefix.1 = (f32[1024,6272]{1,0:T(8,128)S(1)}, f32[1024,128]{1,0:T(8,128)S(1)}, f32[8,1024]{1,0:T(8,128)S(1)}, f32[1,1024]{1,0:T(1,128)S(1)}) custom-call(bf16[1024,512]{1,0:T(8,128)(2,1)} %h_ref.1, bf16[512,25088]{1,0:T(8,128)(2,1)} %w_ref.1, f32[1,1024]{1,0:T(1,128)} %bitcast.3, s32[1,1024]{1,0:T(1,128)} %bitcast.4), custom_call_target="tpu_custom_call" | custom-call | tf_op jit(solution)/shard_map/prefix/pallas_call | solution.py:620
  304.2 8.9 %finish.1 = (f32[1024,6272]{1,0:T(8,128)}, f32[1,1024]{1,0:T(1,128)}) custom-call(f32[1024,6272]{1,0:T(8,128)S(1)} %get-tuple-element.8.c_ref, f32[1024,128]{1,0:T(8,128)S(1)} %get-tuple-element.9.coef_ref, f32[8,1024]{1,0:T(8,128)S(1)} %get-tuple-element.10.factor_ref, f32[1,1024]{1,0:T(1,128)S(1)} %get-tuple-element.11.tgt_ref), custom_call_target="tpu_custom_call" | custom-call | tf_op jit(solution)/shard_map/finish/pallas_call | solution.py:672

commit v3 on v2

--- a/solution.py
+++ b/solution.py
@@ -542,7 +542,7 @@
     slots, n, n_cols = buf.shape
     steps = c_ref.shape[0] // n
     turn = max(n, LANES)
-    tgt_copy = pltpu.make_async_copy(tgt_ref, tgt_out_ref, ends.at[2])
+    tgt_copy = pltpu.make_async_copy(tgt_ref, tgt_out_ref, ends.at[4])
     tgt_copy.start()
 
     def put(i):
@@ -562,24 +562,25 @@
             buf[(*to, span)] = c_ref[at, span] * coef[:, k : k + 1] + coef[:, SLOTS + k : SLOTS + k + 1]
 
     turn_factors(0)
-    half = n // 2
-
-    def put_half(h):
-        at = pl.ds(pl.multiple_of(h * half, half), half)
+    n_parts = 4
+    part = n // n_parts
+
+    def put_part(h):
+        at = pl.ds(pl.multiple_of(h * part, part), part)
         return pltpu.make_async_copy(buf.at[slots - 1, at], out_ref.at[at], ends.at[h])
 
-    @pl.loop(0, 2)
+    @pl.loop(0, n_parts)
     def _(h):
-        at = pl.ds(pl.multiple_of(h * half, half), half)
-        table(at, half, (slots - 1, at))
-        put_half(h).start()
+        at = pl.ds(pl.multiple_of(h * part, part), part)
+        table(at, part, (slots - 1, at))
+        put_part(h).start()
 
     @pl.loop(1, steps)
     def _(i):
         @pl.when(i == slots)
         def _():
-            put_half(0).wait()
-            put_half(1).wait()
+            for h in range(n_parts):
+                put_part(h).wait()
 
         @pl.when(i > slots)
         def _():
@@ -681,7 +682,7 @@
                 pltpu.VMEM((4, n, n_cols), F32),
                 pltpu.VMEM((rows, 8), F32),
                 dma((4,)),
-                dma((3,)),
+                dma((5,)),
             ],
             compiler_params=pltpu.CompilerParams(vmem_limit_bytes=9 << 20),
             name="finish",

time: 313 us -> 314 us (level)
  no operation moved by 1% of the time
where the time goes in v3:
time: 314 us
  Pallas kernels  313 us (100%)
    pallas_call x1, Pallas kernels, local_step(): pl.pallas_call(functools.partial(prefix_kernel, n_cols), out_shape=(pltpu...  304 us
    pallas_call x1, Pallas kernels, local_step(): pl.pallas_call(functools.partial(finish_kernel, tiles, lanes), out_shape=...  9.22 us

profile of v3, /device:TPU:0, one launch (start us, length us, event | category | flops | bytes accessed | tf_op | source)
XLA Modules:
  0.0 313.6 jit_solution(12869538541998194999)
XLA Ops:
  0.6 303.6 %prefix.1 = (f32[1024,6272]{1,0:T(8,128)S(1)}, f32[1024,128]{1,0:T(8,128)S(1)}, f32[8,1024]{1,0:T(8,128)S(1)}, f32[1,1024]{1,0:T(1,128)S(1)}) custom-call(bf16[1024,512]{1,0:T(8,128)(2,1)} %h_ref.1, bf16[512,25088]{1,0:T(8,128)(2,1)} %w_ref.1, f32[1,1024]{1,0:T(1,128)} %bitcast.3, s32[1,1024]{1,0:T(1,128)} %bitcast.4), custom_call_target="tpu_custom_call" | custom-call | tf_op jit(solution)/shard_map/prefix/pallas_call | solution.py:621
  304.2 9.2 %finish.1 = (f32[1024,6272]{1,0:T(8,128)}, f32[1,1024]{1,0:T(1,128)}) custom-call(f32[1024,6272]{1,0:T(8,128)S(1)} %get-tuple-element.8.c_ref, f32[1024,128]{1,0:T(8,128)S(1)} %get-tuple-element.9.coef_ref, f32[8,1024]{1,0:T(8,128)S(1)} %get-tuple-element.10.factor_ref, f32[1,1024]{1,0:T(1,128)S(1)} %get-tuple-element.11.tgt_ref), custom_call_target="tpu_custom_call" | custom-call | tf_op jit(solution)/shard_map/finish/pallas_call | solution.py:673

commit v4 on v2

--- a/solution.py
+++ b/solution.py
@@ -488,7 +488,7 @@
     def _(i):
         at = pl.ds(pl.multiple_of(i * few, few), few)
         coef = coef_ref[at, :]
-        for q in range(folds_of(plan, first_end)[-1][2], n_whole):
+        for q in range(folds_of(plan, first_end)[-1][2], n_whole - 1):
             span = slice(tiles[q][0], sum(tiles[q]))
             c_ref[at, span] = c_ref[at, span] * coef[:, q : q + 1] + coef[:, SLOTS + q : SLOTS + q + 1]
 
@@ -668,7 +668,7 @@
         lanes = list(range(n_tiles))
         for _, g0, g1 in folds_of(plan, first_end):
             lanes[g0:g1] = [g0] * (g1 - g0)
-        lanes[g1 : last_whole + 1] = [SLOTS - 1] * (last_whole + 1 - g1)
+        lanes[g1:last_whole] = [SLOTS - 1] * (last_whole - g1)
         cdf, cdf_tgt = pl.pallas_call(
             functools.partial(finish_kernel, tiles, lanes),
             out_shape=(

time: 313 us -> 313 us (level)
  no operation moved by 1% of the time
where the time goes in v4:
time: 313 us
  Pallas kernels  313 us (100%)
    pallas_call x1, Pallas kernels, local_step(): pl.pallas_call(functools.partial(prefix_kernel, n_cols), out_shape=(pltpu...  304 us
    pallas_call x1, Pallas kernels, local_step(): pl.pallas_call(functools.partial(finish_kernel, tiles, lanes), out_shape=...  8.98 us

profile of v4, /device:TPU:0, one launch (start us, length us, event | category | flops | bytes accessed | tf_op | source)
XLA Modules:
  0.0 313.3 jit_solution(14013134140309646334)
XLA Ops:
  0.6 303.6 %prefix.1 = (f32[1024,6272]{1,0:T(8,128)S(1)}, f32[1024,128]{1,0:T(8,128)S(1)}, f32[8,1024]{1,0:T(8,128)S(1)}, f32[1,1024]{1,0:T(1,128)S(1)}) custom-call(bf16[1024,512]{1,0:T(8,128)(2,1)} %h_ref.1, bf16[512,25088]{1,0:T(8,128)(2,1)} %w_ref.1, f32[1,1024]{1,0:T(1,128)} %bitcast.3, s32[1,1024]{1,0:T(1,128)} %bitcast.4), custom_call_target="tpu_custom_call" | custom-call | tf_op jit(solution)/shard_map/prefix/pallas_call | solution.py:620
  304.2 9.0 %finish.1 = (f32[1024,6272]{1,0:T(8,128)}, f32[1,1024]{1,0:T(1,128)}) custom-call(f32[1024,6272]{1,0:T(8,128)S(1)} %get-tuple-element.8.c_ref, f32[1024,128]{1,0:T(8,128)S(1)} %get-tuple-element.9.coef_ref, f32[8,1024]{1,0:T(8,128)S(1)} %get-tuple-element.10.factor_ref, f32[1,1024]{1,0:T(1,128)S(1)} %get-tuple-element.11.tgt_ref), custom_call_target="tpu_custom_call" | custom-call | tf_op jit(solution)/shard_map/finish/pallas_call | solution.py:672
